TPU v7x, 32 devices: a whole 2x2x4 slice. The times are simulated.
32 devices in a mesh: ep: 8 (over z, x), etp: 4 (over y, core).
Axes of the slice: x: 2, y: 2, z: 4, core: 2. Of those that a mesh axis runs over, the one named last changes fastest.
Arguments:
- tokens: bfloat16 [1024, 4096], P('ep', 'etp'), may hold values from -6 to 6
- expert_ids: int32 [1024, 8], P('ep'), may hold values from 0 to 15, all different within a row; in each aligned block of 128 rows (0 to 127, 128 to 255, ...) at most 96 rows name the same one
- gate_prob: float32 [1024, 8], P('ep'), may hold values from 0.05 to 1
- gate_weight: bfloat16 [16, 4096, 1536], P('ep', None, 'etp'), may hold values from -0.09375 to 0.09375
- up_weight: bfloat16 [16, 4096, 1536], P('ep', None, 'etp'), may hold values from -0.09375 to 0.09375
- down_weight: bfloat16 [16, 1536, 4096], P('ep', 'etp'), may hold values from -0.15625 to 0.15625
Outputs:
- mixed: bfloat16 [1024, 4096], P('ep', 'etp')
Inputs may be any that keep to these rules, and one draw needn't show every extreme that they name: `expert_ids`: each row names 8 different experts. Within each aligned block of 128 rows (one token group) no expert is named more than 96 times, and in every draw some expert is named exactly 96 times in some block.
All inputs are finite; a program needn't handle non-finite values.
Results may differ from a plain program's by a relative error of at most 0.012.
Values may be sent and summed in bfloat16 or wider, within the bound.
A program may use at most 128 MiB of HBM per device.

v0:
```python
import functools

import jax
import jax.numpy as jnp
from jax import lax
from jax.experimental import pallas as pl
from jax.experimental.pallas import tpu as pltpu
from jax.sharding import PartitionSpec as P

MESH = pl.DeviceIdType.MESH
VMEM_BUDGET = 16 << 20


def place(sizes):
    ep, etp = lax.axis_index("ep"), lax.axis_index("etp")
    return (ep // 2, ep % 2, etp // 2, etp % 2)


def flip(at, bits):
    bit = 1
    while bit <= bits:
        if bits & bit:
            at = at + bit - 2 * bit * ((at // bit) % 2)
        bit *= 2
    return at


def moved(here, sizes, rel):
    return tuple(flip(h, r) for h, r in zip(here, rel))


def device(at):
    z, x, y, c = at
    return (z * 2 + x, y * 2 + c)


def barrier(here, sizes, rels):
    sem = pltpu.get_barrier_semaphore()
    for rel in rels:
        pl.semaphore_signal(sem, inc=1, device_id=device(moved(here, sizes, rel)), device_id_type=MESH)
    pl.semaphore_wait(sem, len(rels))


def gather_kernel(sizes, x_ref, w_ref, gate_hbm, up_hbm, hidden_ref, out_ref, w_out_ref,
                  gate_ref, up_ref, send_sem, recv_sem, w_send, w_recv, own_sem, load_sem):
    nz = sizes[0]
    rows, cols = x_ref.shape
    half = rows // 2
    here = place(sizes)
    z_rels = [(d, 0, 0, 0) for d in range(1, nz)]
    ep_rels = [(d, e, 0, 0) for d in range(nz) for e in range(2) if d or e]
    barrier(here, sizes, ep_rels + [(0, 0, 1, 0), (0, 0, 0, 1)])

    def number(rel):
        return ((rel[0] * 2 + rel[1]) * 2 + rel[2]) * 2 + rel[3]

    def slot(h, rel):
        group, member = device(moved(here, sizes, rel))
        return out_ref.at[pl.ds(pl.multiple_of(group * rows + h * half, half), half),
                          pl.ds(pl.multiple_of(member * cols, cols), cols)]

    sends = []

    def send(h, rel, step):
        lands = tuple(r ^ s for r, s in zip(rel, step))
        src = slot(h, rel) if any(rel) else x_ref.at[pl.ds(h * half, half), :]
        copy = pltpu.make_async_remote_copy(
            src_ref=src, dst_ref=slot(h, rel), send_sem=send_sem.at[len(sends)],
            recv_sem=recv_sem.at[h, number(lands)],
            device_id=device(moved(here, sizes, step)), device_id_type=MESH)
        copy.start()
        sends.append(copy)

    def arrive(h, rel):
        ref = slot(h, rel)
        pltpu.make_async_copy(ref, ref, recv_sem.at[h, number(rel)]).wait()

    first = {0: (0, 1, 0, 0), 1: (0, 0, 1, 0)}
    second = {0: (0, 0, 1, 0), 1: (0, 1, 0, 0)}
    other = (0, 0, 0, 1)

    def pass_on(d):
        for h in range(2):
            if d:
                arrive(h, (d, 0, 0, 0))
            send(h, (d, 0, 0, 0), first[h])
            send(h, (d, 0, 0, 0), second[h])
            send(h, (d, 0, 0, 0), other)

    def pass_second(d):
        for h in range(2):
            rel = (d,) + first[h][1:]
            arrive(h, rel)
            send(h, rel, second[h])
            send(h, rel, other)

    def pass_last(d):
        for h in range(2):
            for rel in ((d,) + second[h][1:], (d, 1, 1, 0)):
                arrive(h, rel)
                send(h, rel, other)

    own = pltpu.make_async_copy(
        x_ref, out_ref.at[pl.ds(pl.multiple_of(device(here)[0] * rows, rows), rows),
                          pl.ds(pl.multiple_of(device(here)[1] * cols, cols), cols)], own_sem)
    own.start()
    for step in z_rels[:1]:
        for h in range(2):
            send(h, (0, 0, 0, 0), step)
    pass_on(0)
    for step in z_rels[1:]:
        for h in range(2):
            send(h, (0, 0, 0, 0), step)
    w_sends = []
    me = device(here)[0]
    for i, rel in enumerate(ep_rels):
        copy = pltpu.make_async_remote_copy(
            src_ref=w_ref, dst_ref=w_out_ref.at[me], send_sem=w_send.at[i],
            recv_sem=w_recv.at[i],
            device_id=device(moved(here, sizes, rel)), device_id_type=MESH)
        copy.start()
        w_sends.append(copy)
    w_own = pltpu.make_async_copy(w_ref, w_out_ref.at[me], w_recv.at[len(ep_rels)])
    w_own.start()
    loads = [pltpu.make_async_copy(gate_hbm, gate_ref, load_sem.at[0]),
             pltpu.make_async_copy(up_hbm, up_ref, load_sem.at[1])]
    for load in loads:
        load.start()
    members, units = gate_ref.shape[0], gate_ref.shape[2]

    def compute(d):
        for e in range(2):
            for f in range(2):
                for h in range(2):
                    arrive(h, (d, e, f, 1))
        first_group = flip(here[0], d) * 2
        at = pl.ds(pl.multiple_of(first_group * rows, 2 * rows), 2 * rows)
        x = out_ref[at, :]
        share = w_out_ref[pl.ds(first_group, 2)].reshape(2 * rows, w_ref.shape[1])
        lane = lax.broadcasted_iota(jnp.int32, share.shape, 1)
        for m in range(members):
            scale = jnp.sum(jnp.where(lane == me * members + m, share, 0.0), axis=1, keepdims=True)
            gate = jnp.dot(x, gate_ref[m], preferred_element_type=jnp.float32)
            up = jnp.dot(x, up_ref[m], preferred_element_type=jnp.float32)
            hidden_ref[at, m * units:(m + 1) * units] = (jax.nn.silu(gate) * up * scale).astype(hidden_ref.dtype)

    for d in range(1, nz + 3):
        if d < nz:
            pass_on(d)
        if d <= nz:
            pass_second(d - 1)
        if d == 3:
            for i in range(len(ep_rels)):
                w_sends[i].wait_send()
                ref = w_out_ref.at[0]
                pltpu.make_async_copy(ref, ref, w_recv.at[i]).wait()
            own.wait()
            w_own.wait()
            for load in loads:
                load.wait()
        if d >= 3:
            compute(d - 3)
        if 2 <= d <= nz + 1:
            pass_last(d - 2)
    for copy in sends:
        copy.wait_send()


def gather(sizes, x, w, gate, up):
    groups, parts = sizes[0] * sizes[1], sizes[2] * sizes[3]
    rows, cols = x.shape
    n_send = 2 * (sizes[0] - 1 + sizes[0] + 2 * sizes[0] + 4 * sizes[0])
    return pl.pallas_call(
        functools.partial(gather_kernel, sizes),
        out_shape=jax.ShapeDtypeStruct((groups * rows, gate.shape[0] * gate.shape[2]), x.dtype),
        in_specs=[pl.BlockSpec(memory_space=pltpu.VMEM)] * 2 + [pl.BlockSpec(memory_space=pl.ANY)] * 2,
        out_specs=pl.BlockSpec(memory_space=pltpu.VMEM),
        scratch_shapes=[
            pltpu.VMEM((groups * rows, parts * cols), x.dtype),
            pltpu.VMEM((groups,) + w.shape, w.dtype),
            pltpu.VMEM(gate.shape, gate.dtype),
            pltpu.VMEM(up.shape, up.dtype),
            pltpu.SemaphoreType.DMA((n_send,)),
            pltpu.SemaphoreType.DMA((2, groups * parts)),
            pltpu.SemaphoreType.DMA((groups - 1,)),
            pltpu.SemaphoreType.DMA((groups,)),
            pltpu.SemaphoreType.DMA,
            pltpu.SemaphoreType.DMA((2,)),
        ],
        compiler_params=pltpu.CompilerParams(collective_id=0, has_side_effects=True, vmem_limit_bytes=58 << 20),
        name="gather_hidden",
    )(x, w, gate, up)


def scatter_kernel(sizes, p_ref, out_ref, buf_c, buf_1, buf_2, buf_z, send_sem, recv_c, recv_1, recv_2, recv_z):
    nz = sizes[0]
    rows, cols = out_ref.shape
    half = rows // 2
    here = place(sizes)
    barrier(here, sizes, [(d, 0, 0, 0) for d in range(1, nz)] + [(0, 1, 0, 0), (0, 0, 1, 0), (0, 0, 0, 1)])
    axis = ((0, 1, 0, 0), (0, 0, 1, 0))
    first = {0: axis[1], 1: axis[0]}
    second = {0: axis[0], 1: axis[1]}
    sends = []

    def local(h, rel):
        group, member = device(moved(here, sizes, rel))
        return p_ref.at[pl.ds(pl.multiple_of(group * rows + h * half, half), half),
                        pl.ds(pl.multiple_of(member * cols, cols), cols)]

    def rel_of(h, a, b, d):
        e, f = (b, a) if h == 0 else (a, b)
        return (d, e, f)

    def send(src, dst, recv, step):
        copy = pltpu.make_async_remote_copy(
            src_ref=src, dst_ref=dst, send_sem=send_sem.at[len(sends)], recv_sem=recv,
            device_id=device(moved(here, sizes, step)), device_id_type=MESH)
        copy.start()
        sends.append(copy)

    def arrive(ref, sem):
        pltpu.make_async_copy(ref, ref, sem).wait()

    def add(dst, *srcs):
        chunk = 16

        @pl.loop(0, half // chunk)
        def _(i):
            at = pl.ds(pl.multiple_of(i * chunk, chunk), chunk)
            total = srcs[0][at, :].astype(jnp.float32)
            for src in srcs[1:]:
                total = total + src[at, :].astype(jnp.float32)
            dst[at, :] = total.astype(dst.dtype)

    zs = list(range(nz))[::-1]
    for d in zs:
        for a, b in ((1, 1), (1, 0), (0, 1), (0, 0)):
            for h in range(2):
                send(local(h, rel_of(h, a, b, d) + (1,)), buf_c.at[h, a, b, d], recv_c.at[h, a, b, d], (0, 0, 0, 1))

    def step_first(d):
        for b in (1, 0):
            for h in range(2):
                piece = buf_c.at[h, 1, b, d]
                arrive(piece, recv_c.at[h, 1, b, d])
                add(piece, piece, local(h, rel_of(h, 1, b, d) + (0,)))
                send(piece, buf_1.at[h, b, d], recv_1.at[h, b, d], first[h])

    def step_second(d):
        for h in range(2):
            piece = buf_c.at[h, 0, 1, d]
            arrive(piece, recv_c.at[h, 0, 1, d])
            arrive(buf_1.at[h, 1, d], recv_1.at[h, 1, d])
            add(piece, piece, local(h, rel_of(h, 0, 1, d) + (0,)), buf_1.at[h, 1, d])
            send(piece, buf_2.at[h, d], recv_2.at[h, d], second[h])

    def step_last(d):
        for h in range(2):
            piece = buf_c.at[h, 0, 0, d]
            arrive(piece, recv_c.at[h, 0, 0, d])
            arrive(buf_1.at[h, 0, d], recv_1.at[h, 0, d])
            arrive(buf_2.at[h, d], recv_2.at[h, d])
            srcs = (piece, local(h, rel_of(h, 0, 0, d) + (0,)), buf_1.at[h, 0, d], buf_2.at[h, d])
            if d:
                add(piece, *srcs)
                send(piece, buf_z.at[h, d - 1], recv_z.at[h, d - 1], (d, 0, 0, 0))
            else:
                for k in range(nz - 1):
                    arrive(buf_z.at[h, k], recv_z.at[h, k])
                add(out_ref.at[pl.ds(h * half, half), :], *srcs, *[buf_z.at[h, k] for k in range(nz - 1)])

    for i in range(nz + 2):
        if i < nz:
            step_first(zs[i])
        if 1 <= i <= nz:
            step_second(zs[i - 1])
        if i >= 2:
            step_last(zs[i - 2])
    for copy in sends:
        copy.wait_send()


def scatter(sizes, p):
    nz = sizes[0]
    groups, parts = nz * 2, sizes[2] * sizes[3]
    rows, cols = p.shape[0] // groups, p.shape[1] // parts
    half = rows // 2
    n_send = 2 * (4 * nz + 2 * nz + nz + nz - 1)
    return pl.pallas_call(
        functools.partial(scatter_kernel, sizes),
        out_shape=jax.ShapeDtypeStruct((rows, cols), p.dtype),
        in_specs=[pl.BlockSpec(memory_space=pltpu.VMEM)],
        out_specs=pl.BlockSpec(memory_space=pltpu.VMEM),
        scratch_shapes=[
            pltpu.VMEM((2, 2, 2, nz, half, cols), p.dtype),
            pltpu.VMEM((2, 2, nz, half, cols), p.dtype),
            pltpu.VMEM((2, nz, half, cols), p.dtype),
            pltpu.VMEM((2, nz - 1, half, cols), p.dtype),
            pltpu.SemaphoreType.DMA((n_send,)),
            pltpu.SemaphoreType.DMA((2, 2, 2, nz)),
            pltpu.SemaphoreType.DMA((2, 2, nz)),
            pltpu.SemaphoreType.DMA((2, nz)),
            pltpu.SemaphoreType.DMA((2, nz - 1)),
        ],
        compiler_params=pltpu.CompilerParams(collective_id=1, has_side_effects=True, vmem_limit_bytes=40 << 20),
        name="reduce_scatter",
    )(p)


def hidden_kernel(x_ref, w_ref, gate_ref, up_ref, out_ref):
    gate = jnp.dot(x_ref[...], gate_ref[0], preferred_element_type=jnp.float32)
    up = jnp.dot(x_ref[...], up_ref[0], preferred_element_type=jnp.float32)
    out_ref[...] = (jax.nn.silu(gate) * up * w_ref[0]).astype(out_ref.dtype)


def down_kernel(h_ref, down_ref, out_ref):
    out_ref[...] = jnp.dot(h_ref[...], down_ref[...], preferred_element_type=jnp.float32).astype(out_ref.dtype)


def tile_of(total, wanted):
    while total % wanted:
        wanted //= 2
    return wanted


def hidden_units(x, scale, gate_weight, up_weight):
    members, width, units = gate_weight.shape
    rows = x.shape[0]
    tile = tile_of(rows, 256)
    return pl.pallas_call(
        hidden_kernel,
        grid=(members, rows // tile),
        out_shape=jax.ShapeDtypeStruct((rows, members * units), x.dtype),
        in_specs=[
            pl.BlockSpec((tile, width), lambda e, m: (m, 0)),
            pl.BlockSpec((1, tile, 1), lambda e, m: (e, m, 0)),
            pl.BlockSpec((1, width, units), lambda e, m: (e, 0, 0)),
            pl.BlockSpec((1, width, units), lambda e, m: (e, 0, 0)),
        ],
        out_specs=pl.BlockSpec((tile, units), lambda e, m: (m, e)),
        compiler_params=pltpu.CompilerParams(vmem_limit_bytes=40 << 20),
        name="hidden",
    )(x, scale, gate_weight, up_weight)


def down_product(hidden, down_weight):
    members, units, width = down_weight.shape
    rows = hidden.shape[0]
    down = down_weight.reshape(members * units, width)
    tile_n = tile_of(width, 512)
    tile_m = tile_of(rows, 1024)
    return pl.pallas_call(
        down_kernel,
        grid=(rows // tile_m, width // tile_n),
        out_shape=jax.ShapeDtypeStruct((rows, width), hidden.dtype),
        in_specs=[
            pl.BlockSpec((tile_m, members * units), lambda m, n: (m, 0)),
            pl.BlockSpec((members * units, tile_n), lambda m, n: (0, n)),
        ],
        out_specs=pl.BlockSpec((tile_m, tile_n), lambda m, n: (m, n)),
        compiler_params=pltpu.CompilerParams(vmem_limit_bytes=50 << 20),
        name="down",
    )(hidden, down)


def body(tokens, expert_ids, gate_prob, gate_weight, up_weight, down_weight):
    groups, parts = lax.axis_size("ep"), lax.axis_size("etp")
    members = gate_weight.shape[0]
    numbers = jnp.arange(members * groups, dtype=jnp.int32)
    share = jnp.sum(jnp.where(expert_ids[:, :, None] == numbers, gate_prob[:, :, None], 0.0), axis=1)
    size = groups * parts * tokens.size * tokens.dtype.itemsize
    kernels = groups > 2 and groups & (groups - 1) == 0 and parts == 4 and size <= VMEM_BUDGET
    sizes = (groups // 2, 2, parts // 2, 2)
    if kernels:
        hidden = gather(sizes, tokens, share, gate_weight, up_weight)
        return scatter(sizes, down_product(hidden, down_weight))
    gathered = lax.all_gather(lax.all_gather(tokens, "ep", axis=0, tiled=True), "etp", axis=1, tiled=True)
    shares = lax.all_gather(share, "ep", axis=0, tiled=True)
    mine = lax.dynamic_slice_in_dim(shares, lax.axis_index("ep") * members, members, axis=1)
    hidden = hidden_units(gathered, jnp.transpose(mine)[:, :, None], gate_weight, up_weight)
    partial_sum = down_product(hidden, down_weight)
    summed = lax.psum_scatter(partial_sum, "etp", scatter_dimension=1, tiled=True)
    return lax.psum_scatter(summed, "ep", scatter_dimension=0, tiled=True)


def solution(mesh):
    in_specs = (
        P("ep", "etp"),
        P("ep", None),
        P("ep", None),
        P("ep", None, "etp"),
        P("ep", None, "etp"),
        P("ep", "etp", None),
    )
    out_specs = P("ep", "etp")
    return jax.shard_map(body, mesh=mesh, in_specs=in_specs, out_specs=out_specs, check_vma=False)
```

profile of v0, /device:TPU:0, one launch (start us, length us, event | category | flops | bytes accessed | tf_op | source)
XLA Modules:
  0.0 134.2 jit_solution(4753130802519986512)
XLA Ops:
  0.0 0.7 select_reduce_fusion
  0.7 0.7 copy.9.w_ref
  1.4 64.4 %gather_hidden.1.h_ref = bf16[1024,768]{1,0:T(8,128)(2,1)} custom-call(bf16[128,1024]{1,0:T(8,128)(2,1)} %x_ref.1, f32[128,16]{1,0:T(8,128)} %copy.9.w_ref, bf16[2,4096,384]{2,1,0:T(8,128)(2,1)} %gate_hbm.1, bf16[2,4096,384]{2,1,0:T(8,128)(2,1)} %up_hbm.1), custom_call_target="tpu_custom_call" | custom-call | tf_op jit(solution)/shard_map/gather_hidden/pallas_call | solution.py:173
  65.9 0.0 copy-start.1
  65.9 1.4 %copy-done.1 = bf16[1024,768]{1,0:T(8,128)(2,1)S(1)} copy-done((bf16[1024,768]{1,0:T(8,128)(2,1)S(1)}, bf16[1024,768]{1,0:T(8,128)(2,1)}, u32[]{:S(2)}) %copy-start.1) | copy-done | bytes 1572888
  67.3 11.8 %down.1.p_ref = bf16[1024,4096]{1,0:T(8,128)(2,1)} custom-call(bf16[1024,768]{1,0:T(8,128)(2,1)S(1)} %copy-done.1, bf16[768,4096]{1,0:T(8,128)(2,1)} %bitcast.1), custom_call_target="tpu_custom_call" | custom-call | tf_op jit(solution)/shard_map/down/pallas_call | solution.py:353
  79.1 0.0 copy-start
  79.1 3.4 %copy-done = bf16[1024,4096]{1,0:T(8,128)(2,1)S(1)} copy-done((bf16[1024,4096]{1,0:T(8,128)(2,1)S(1)}, bf16[1024,4096]{1,0:T(8,128)(2,1)}, u32[]{:S(2)}) %copy-start) | copy-done | bytes 8388632
  82.4 51.1 %reduce_scatter.1 = bf16[128,1024]{1,0:T(8,128)(2,1)S(1)} custom-call(bf16[1024,4096]{1,0:T(8,128)(2,1)S(1)} %copy-done), custom_call_target="tpu_custom_call" | custom-call | tf_op jit(solution)/shard_map/reduce_scatter/pallas_call | solution.py:290
  133.5 0.7 copy.11
Async XLA Ops:
  65.9 1.4 %copy-start.1 = (bf16[1024,768]{1,0:T(8,128)(2,1)S(1)}, bf16[1024,768]{1,0:T(8,128)(2,1)}, u32[]{:S(2)}) copy-start(bf16[1024,768]{1,0:T(8,128)(2,1)} %gather_hidden.1.h_ref) | copy-start | bytes 4718596
  79.1 3.4 %copy-start = (bf16[1024,4096]{1,0:T(8,128)(2,1)S(1)}, bf16[1024,4096]{1,0:T(8,128)(2,1)}, u32[]{:S(2)}) copy-start(bf16[1024,4096]{1,0:T(8,128)(2,1)} %down.1.p_ref) | copy-start | bytes 25165828
where the time goes:
time: 135 us; the launch traced here: 134 us
  Pallas kernels  127 us (94%)
  local copies, waits for them, and re-layouts  6.22 us (5%)
    pallas_call x1, Pallas kernels, gather(): pl.pallas_call(functools.partial(gather_kernel, sizes), out_shape=jax.Sha...  64.4 us
    pallas_call x1, Pallas kernels, scatter(): pl.pallas_call(functools.partial(scatter_kernel, sizes), out_shape=jax.Sh...  51.1 us
    pallas_call x1, Pallas kernels, down_product(): pl.pallas_call(down_kernel, grid=(rows // tile_m, width // tile_n), out_s...  11.8 us
    unnamed x5, local copies, waits for them, and re-layouts  5.49 us

commit v1 on v0

v1 whole, which is shorter than its diff:
```python
import functools
import math

import jax
import jax.numpy as jnp
from jax import lax
from jax.experimental import pallas as pl
from jax.experimental.pallas import tpu as pltpu
from jax.sharding import PartitionSpec as P

MESH = pl.DeviceIdType.MESH
VMEM_BUDGET = 56 << 20


def place(sizes):
    ep, etp = lax.axis_index("ep"), lax.axis_index("etp")
    return (ep // 2, ep % 2, etp // 2, etp % 2)


def flip(at, bits):
    bit = 1
    while bit <= bits:
        if bits & bit:
            at = at + bit - 2 * bit * ((at // bit) % 2)
        bit *= 2
    return at


def moved(here, sizes, rel):
    return tuple(flip(h, r) for h, r in zip(here, rel))


def device(at):
    z, x, y, c = at
    return (z * 2 + x, y * 2 + c)


def layer_kernel(sizes, x_hbm, ids_hbm, prob_hbm, gate_hbm, up_hbm, down_hbm, out_ref,
                 x_ref, ids_ref, prob_ref, own_share, share_ref, w_ref, down_ref, hid_ref, part_ref,
                 buf_c, buf_1, buf_2, buf_z,
                 load_sem, send_sem, x_recv, share_recv, recv_c, recv_1, recv_2, recv_z):
    nz = sizes[0]
    rows, cols = x_hbm.shape
    half = rows // 2
    members, width, units = gate_hbm.shape
    experts = own_share.shape[0]
    here = place(sizes)
    z, x, y, c = here
    me = device(here)[0]
    axis = ((0, 1, 0, 0), (0, 0, 1, 0))
    other = (0, 0, 0, 1)
    ep_rels = [(d, e, 0, 0) for d in range(nz) for e in range(2) if d or e]
    greeted = ep_rels + [axis[1], other]

    sem = pltpu.get_barrier_semaphore()
    for rel in greeted:
        pl.semaphore_signal(sem, inc=1, device_id=device(moved(here, sizes, rel)), device_id_type=MESH)

    def number(rel):
        return ((rel[0] * 2 + rel[1]) * 2 + rel[2]) * 2 + rel[3]

    def slot(h, rel):
        group, member = device(moved(here, sizes, rel))
        return x_ref.at[pl.ds(pl.multiple_of(group * rows + h * half, half), half),
                        pl.ds(pl.multiple_of(member * cols, cols), cols)]

    own = pltpu.make_async_copy(
        x_hbm, x_ref.at[pl.ds(pl.multiple_of(me * rows, rows), rows),
                        pl.ds(pl.multiple_of(device(here)[1] * cols, cols), cols)], load_sem.at[0])
    ids = pltpu.make_async_copy(ids_hbm, ids_ref, load_sem.at[1])
    prob = pltpu.make_async_copy(prob_hbm, prob_ref, load_sem.at[2])
    for load in (own, ids, prob):
        load.start()
    loads = []
    for m in range(members):
        loads.append(pltpu.make_async_copy(gate_hbm.at[m], w_ref.at[m, :, pl.ds(0, units)], load_sem.at[3 + 3 * m]))
        loads.append(pltpu.make_async_copy(up_hbm.at[m], w_ref.at[m, :, pl.ds(units, units)], load_sem.at[4 + 3 * m]))
    for m in range(members):
        loads.append(pltpu.make_async_copy(down_hbm.at[m], down_ref.at[pl.ds(m * units, units), :], load_sem.at[5 + 3 * m]))
    for load in loads:
        load.start()

    ids.wait()
    prob.wait()
    expert = lax.broadcasted_iota(jnp.int32, (experts, rows), 0)
    share = jnp.zeros((experts, rows), jnp.float32)
    for k in range(ids_ref.shape[0]):
        share = share + jnp.where(expert == ids_ref[k:k + 1, :], prob_ref[k:k + 1, :], 0.0)
    own_share[...] = share
    own.wait()
    pl.semaphore_wait(sem, len(greeted))

    sends = []

    def push(src, dst, recv, step):
        copy = pltpu.make_async_remote_copy(
            src_ref=src, dst_ref=dst, send_sem=send_sem.at[len(sends)], recv_sem=recv,
            device_id=device(moved(here, sizes, step)), device_id_type=MESH)
        copy.start()
        sends.append(copy)

    def arrive(ref, recv):
        pltpu.make_async_copy(ref, ref, recv).wait()

    def send(h, rel, step):
        lands = tuple(r ^ s for r, s in zip(rel, step))
        push(slot(h, rel), slot(h, rel), x_recv.at[h, number(lands)], step)

    def landed(h, rel):
        arrive(slot(h, rel), x_recv.at[h, number(rel)])

    first = {0: axis[0], 1: axis[1]}
    second = {0: axis[1], 1: axis[0]}

    def pass_on(d, h):
        if d:
            landed(h, (d, 0, 0, 0))
        send(h, (d, 0, 0, 0), first[h])
        send(h, (d, 0, 0, 0), second[h])
        send(h, (d, 0, 0, 0), other)

    def pass_second(d):
        for h in range(2):
            rel = (d,) + first[h][1:]
            landed(h, rel)
            send(h, rel, second[h])
            send(h, rel, other)

    def pass_last(d):
        for h in range(2):
            for rel in ((d,) + second[h][1:], (d, 1, 1, 0)):
                landed(h, rel)
                send(h, rel, other)

    def whole(d):
        for h in range(2):
            for e in range(2):
                for f in range(2):
                    landed(h, (d, e, f, 1))

    eye = lax.broadcasted_iota(jnp.int32, (rows, rows), 0) == lax.broadcasted_iota(jnp.int32, (rows, rows), 1)

    def hidden(d, e):
        group = flip(z, d) * 2 + flip(x, e)
        block = x_ref[pl.ds(pl.multiple_of(group * rows, rows), rows), :]

        @pl.loop(0, members)
        def _(m):
            line = share_ref[group, pl.ds(me * members + m, 1), :]
            scale = jnp.sum(jnp.where(eye, jnp.broadcast_to(line, (rows, rows)), 0.0), axis=1, keepdims=True)
            both = jnp.dot(block, w_ref[m], preferred_element_type=jnp.float32)
            gate, up = both[:, :units], both[:, units:]
            hid_ref[d, e * rows:(e + 1) * rows, pl.ds(pl.multiple_of(m * units, 128), units)] = (
                jax.nn.silu(gate) * up * scale).astype(hid_ref.dtype)

    def down(d, g):
        @pl.loop(0, 2)
        def _(f):
            member = (y + f - 2 * y * f) * 2 + flip(c, g)
            at = pl.ds(pl.multiple_of(member * cols, cols), cols)
            part_ref[d, f, g] = jnp.dot(
                hid_ref[d], down_ref[:, at], preferred_element_type=jnp.float32).astype(part_ref.dtype)

    def rel_of(h, a, b):
        return (b, a) if h == 0 else (a, b)

    def local(h, a, b, d, g):
        e, f = rel_of(h, a, b)
        return part_ref.at[d, f, g, pl.ds(e * rows + h * half, half), :]

    out_first = {0: axis[1], 1: axis[0]}
    out_second = {0: axis[0], 1: axis[1]}

    def swap(d):
        for a, b in ((1, 1), (1, 0), (0, 1), (0, 0)):
            for h in range(2):
                push(local(h, a, b, d, 1), buf_c.at[h, a, b, d], recv_c.at[h, a, b, d], other)

    def add(dst, *srcs):
        chunk = 16

        @pl.loop(0, half // chunk)
        def _(i):
            at = pl.ds(pl.multiple_of(i * chunk, chunk), chunk)
            total = srcs[0][at, :].astype(jnp.float32)
            for src in srcs[1:]:
                total = total + src[at, :].astype(jnp.float32)
            dst[at, :] = total.astype(dst.dtype)

    def step_first(d):
        for b in (1, 0):
            for h in range(2):
                piece = buf_c.at[h, 1, b, d]
                arrive(piece, recv_c.at[h, 1, b, d])
                add(piece, piece, local(h, 1, b, d, 0))
                push(piece, buf_1.at[h, b, d], recv_1.at[h, b, d], out_first[h])

    def step_second(d):
        for h in range(2):
            piece = buf_c.at[h, 0, 1, d]
            arrive(piece, recv_c.at[h, 0, 1, d])
            arrive(buf_1.at[h, 1, d], recv_1.at[h, 1, d])
            add(piece, piece, local(h, 0, 1, d, 0), buf_1.at[h, 1, d])
            push(piece, buf_2.at[h, d], recv_2.at[h, d], out_second[h])

    def step_last(d):
        for h in range(2):
            piece = buf_c.at[h, 0, 0, d]
            arrive(piece, recv_c.at[h, 0, 0, d])
            arrive(buf_1.at[h, 0, d], recv_1.at[h, 0, d])
            arrive(buf_2.at[h, d], recv_2.at[h, d])
            srcs = (piece, local(h, 0, 0, d, 0), buf_1.at[h, 0, d], buf_2.at[h, d])
            if d:
                add(piece, *srcs)
                push(piece, buf_z.at[h, d - 1], recv_z.at[h, d - 1], (d, 0, 0, 0))
            else:
                for k in range(nz - 1):
                    arrive(buf_z.at[h, k], recv_z.at[h, k])
                add(out_ref.at[pl.ds(h * half, half), :], *srcs, *[buf_z.at[h, k] for k in range(nz - 1)])

    def send_far(d):
        for h in range(2):
            send(h, (0, 0, 0, 0), (d, 0, 0, 0))

    send_far(1)
    for h in range(2):
        pass_on(0, h)
    for i, rel in enumerate(ep_rels):
        push(own_share, share_ref.at[me], share_recv.at[i], rel)
    keep = pltpu.make_async_copy(own_share, share_ref.at[me], load_sem.at[3 + 3 * members])
    keep.start()
    for d in range(2, nz):
        send_far(d)
    pass_second(0)
    for h in range(2):
        pass_on(1, h)
    pass_last(0)
    for load in loads:
        load.wait()
    keep.wait()
    for i in range(len(ep_rels)):
        arrive(share_ref.at[0], share_recv.at[i])

    last = nz - 1
    for d in range(nz):
        whole(d)
        hidden(d, 0)
        if d < last:
            pass_second(d + 1)
        elif last > 2:
            step_second(last - 1)
        hidden(d, 1)
        if d + 2 < nz:
            for h in range(2):
                pass_on(d + 2, h)
        if d >= 2:
            down(d, 1)
            swap(d)
            down(d, 0)
            step_first(d)
        if d < last:
            pass_last(d + 1)
    step_last(last - 1)
    down(1, 1)
    swap(1)
    down(1, 0)
    step_second(last)
    step_first(1)
    down(0, 1)
    swap(0)
    down(0, 0)
    step_last(last)
    step_second(1)
    step_first(0)
    step_last(1)
    step_second(0)
    step_last(0)
    for copy in sends:
        copy.wait_send()


def layer_scratch(sizes, x, ids, prob, gate, down):
    nz = sizes[0]
    groups, parts = nz * sizes[1], sizes[2] * sizes[3]
    rows, cols = x.shape
    half = rows // 2
    members, width, units = gate.shape
    experts = groups * members
    n_send = 2 * (nz - 1 + 7 * nz) + groups - 1 + 2 * (4 * nz + 2 * nz + nz + nz - 1)
    buffers = [
        pltpu.VMEM((groups * rows, parts * cols), x.dtype),
        pltpu.VMEM(ids.shape, ids.dtype),
        pltpu.VMEM(prob.shape, prob.dtype),
        pltpu.VMEM((experts, rows), prob.dtype),
        pltpu.VMEM((groups, experts, rows), prob.dtype),
        pltpu.VMEM((members, width, 2 * units), gate.dtype),
        pltpu.VMEM((members * units, parts * cols), down.dtype),
        pltpu.VMEM((nz, 2 * rows, members * units), x.dtype),
        pltpu.VMEM((nz, 2, 2, 2 * rows, cols), x.dtype),
        pltpu.VMEM((2, 2, 2, nz, half, cols), x.dtype),
        pltpu.VMEM((2, 2, nz, half, cols), x.dtype),
        pltpu.VMEM((2, nz, half, cols), x.dtype),
        pltpu.VMEM((2, nz - 1, half, cols), x.dtype),
    ]
    semaphores = [
        pltpu.SemaphoreType.DMA((4 + 3 * members,)),
        pltpu.SemaphoreType.DMA((n_send,)),
        pltpu.SemaphoreType.DMA((2, groups * parts)),
        pltpu.SemaphoreType.DMA((groups - 1,)),
        pltpu.SemaphoreType.DMA((2, 2, 2, nz)),
        pltpu.SemaphoreType.DMA((2, 2, nz)),
        pltpu.SemaphoreType.DMA((2, nz)),
        pltpu.SemaphoreType.DMA((2, nz - 1)),
    ]
    return buffers, semaphores


def layer(sizes, x, ids, prob, gate, up, down):
    buffers, semaphores = layer_scratch(sizes, x, ids, prob, gate, down)
    return pl.pallas_call(
        functools.partial(layer_kernel, sizes),
        out_shape=jax.ShapeDtypeStruct(x.shape, x.dtype),
        in_specs=[pl.BlockSpec(memory_space=pl.ANY)] * 6,
        out_specs=pl.BlockSpec(memory_space=pltpu.VMEM),
        scratch_shapes=buffers + semaphores,
        compiler_params=pltpu.CompilerParams(collective_id=0, has_side_effects=True, vmem_limit_bytes=60 << 20),
        name="layer",
    )(x, ids, prob, gate, up, down)


def hidden_kernel(x_ref, w_ref, gate_ref, up_ref, out_ref):
    gate = jnp.dot(x_ref[...], gate_ref[0], preferred_element_type=jnp.float32)
    up = jnp.dot(x_ref[...], up_ref[0], preferred_element_type=jnp.float32)
    out_ref[...] = (jax.nn.silu(gate) * up * w_ref[0]).astype(out_ref.dtype)


def down_kernel(h_ref, down_ref, out_ref):
    out_ref[...] = jnp.dot(h_ref[...], down_ref[...], preferred_element_type=jnp.float32).astype(out_ref.dtype)


def tile_of(total, wanted):
    while total % wanted:
        wanted //= 2
    return wanted


def hidden_units(x, scale, gate_weight, up_weight):
    members, width, units = gate_weight.shape
    rows = x.shape[0]
    tile = tile_of(rows, 256)
    return pl.pallas_call(
        hidden_kernel,
        grid=(members, rows // tile),
        out_shape=jax.ShapeDtypeStruct((rows, members * units), x.dtype),
        in_specs=[
            pl.BlockSpec((tile, width), lambda e, m: (m, 0)),
            pl.BlockSpec((1, tile, 1), lambda e, m: (e, m, 0)),
            pl.BlockSpec((1, width, units), lambda e, m: (e, 0, 0)),
            pl.BlockSpec((1, width, units), lambda e, m: (e, 0, 0)),
        ],
        out_specs=pl.BlockSpec((tile, units), lambda e, m: (m, e)),
        compiler_params=pltpu.CompilerParams(vmem_limit_bytes=40 << 20),
        name="hidden",
    )(x, scale, gate_weight, up_weight)


def down_product(hidden, down_weight):
    members, units, width = down_weight.shape
    rows = hidden.shape[0]
    down = down_weight.reshape(members * units, width)
    tile_n = tile_of(width, 512)
    tile_m = tile_of(rows, 1024)
    return pl.pallas_call(
        down_kernel,
        grid=(rows // tile_m, width // tile_n),
        out_shape=jax.ShapeDtypeStruct((rows, width), hidden.dtype),
        in_specs=[
            pl.BlockSpec((tile_m, members * units), lambda m, n: (m, 0)),
            pl.BlockSpec((members * units, tile_n), lambda m, n: (0, n)),
        ],
        out_specs=pl.BlockSpec((tile_m, tile_n), lambda m, n: (m, n)),
        compiler_params=pltpu.CompilerParams(vmem_limit_bytes=50 << 20),
        name="down",
    )(hidden, down)


def body(tokens, expert_ids, gate_prob, gate_weight, up_weight, down_weight):
    groups, parts = lax.axis_size("ep"), lax.axis_size("etp")
    members = gate_weight.shape[0]
    sizes = (groups // 2, 2, parts // 2, 2)
    rows = tokens.shape[0]
    square = groups > 4 and groups & (groups - 1) == 0 and parts == 4 and members * groups <= rows == 128
    if square:
        ids, prob = jnp.transpose(expert_ids), jnp.transpose(gate_prob)
        buffers = layer_scratch(sizes, tokens, ids, prob, gate_weight, down_weight)[0]
        size = sum(math.prod(b.shape) * b.dtype.itemsize for b in buffers)
        if size <= VMEM_BUDGET:
            return layer(sizes, tokens, ids, prob, gate_weight, up_weight, down_weight)
    numbers = jnp.arange(members * groups, dtype=jnp.int32)
    share = jnp.sum(jnp.where(expert_ids[:, :, None] == numbers, gate_prob[:, :, None], 0.0), axis=1)
    gathered = lax.all_gather(lax.all_gather(tokens, "ep", axis=0, tiled=True), "etp", axis=1, tiled=True)
    shares = lax.all_gather(share, "ep", axis=0, tiled=True)
    mine = lax.dynamic_slice_in_dim(shares, lax.axis_index("ep") * members, members, axis=1)
    hidden = hidden_units(gathered, jnp.transpose(mine)[:, :, None], gate_weight, up_weight)
    partial_sum = down_product(hidden, down_weight)
    summed = lax.psum_scatter(partial_sum, "etp", scatter_dimension=1, tiled=True)
    return lax.psum_scatter(summed, "ep", scatter_dimension=0, tiled=True)


def solution(mesh):
    in_specs = (
        P("ep", "etp"),
        P("ep", None),
        P("ep", None),
        P("ep", None, "etp"),
        P("ep", None, "etp"),
        P("ep", "etp", None),
    )
    out_specs = P("ep", "etp")
    return jax.shard_map(body, mesh=mesh, in_specs=in_specs, out_specs=out_specs, check_vma=False)
```

time: 135 us -> 90 us (0.67)
  Pallas kernels: 127 us -> 88.2 us
  local copies, waits for them, and re-layouts: 6.22 us -> 1.67 us
    pallas_call x3 -> x1, Pallas kernels: 127 us -> 88.2 us  [layer(): pl.pallas_call(functools.partial(layer_kernel, sizes), out_shape=jax.Shap...]
    unnamed x5 -> x1, local copies, waits for them, and re-layouts: 5.49 us -> 1.67 us
where the time goes in v1:
time: 90 us; the launch traced here: 89.9 us
  Pallas kernels  88.2 us (98%)
  local copies, waits for them, and re-layouts  1.67 us (2%)
    pallas_call x1, Pallas kernels, layer(): pl.pallas_call(functools.partial(layer_kernel, sizes), out_shape=jax.Shap...  88.2 us

profile of v1, /device:TPU:0, one launch (start us, length us, event | category | flops | bytes accessed | tf_op | source)
XLA Modules:
  0.0 89.9 jit_solution(3259888660714539252)
XLA Ops:
  0.0 88.2 %layer.1 = bf16[128,1024]{1,0:T(8,128)(2,1)} custom-call(bf16[128,1024]{1,0:T(8,128)(2,1)} %x_hbm.1, s32[8,128]{1,0:T(8,128)} %bitcast.2, f32[8,128]{1,0:T(8,128)} %bitcast.3, bf16[2,4096,384]{2,1,0:T(8,128)(2,1)} %gate_hbm.1, bf16[2,4096,384]{2,1,0:T(8,128)(2,1)} %up_hbm.1, bf16[2,384,4096]{2,1,0:T(8,128)(2,1)} %down_hbm.1), custom_call_target="tpu_custom_call" | custom-call | tf_op jit(solution)/shard_map/layer/pallas_call | solution.py:320
  88.2 1.7 %copy.8 = bf16[128,1024]{1,0:T(8,128)(2,1)} copy(bf16[128,1024]{1,0:T(8,128)(2,1)} %layer.1) | data formatting | bytes 524288

commit v2 on v1

--- a/solution.py
+++ b/solution.py
@@ -37,11 +37,11 @@
 
 def layer_kernel(sizes, x_hbm, ids_hbm, prob_hbm, gate_hbm, up_hbm, down_hbm, out_ref,
                  x_ref, ids_ref, prob_ref, own_share, share_ref, w_ref, down_ref, hid_ref, part_ref,
-                 buf_c, buf_1, buf_2, buf_z,
-                 load_sem, send_sem, x_recv, share_recv, recv_c, recv_1, recv_2, recv_z):
+                 buf_c, buf_1, buf_2, buf_z, late_c, late_zs, late_1, late_2, scale_ref,
+                 load_sem, send_sem, x_recv, share_recv, recv_c, recv_1, recv_2, recv_z,
+                 recv_lc, recv_lz, recv_l1, recv_l2):
     nz = sizes[0]
     rows, cols = x_hbm.shape
-    half = rows // 2
     members, width, units = gate_hbm.shape
     experts = own_share.shape[0]
     here = place(sizes)
@@ -56,12 +56,20 @@
     for rel in greeted:
         pl.semaphore_signal(sem, inc=1, device_id=device(moved(here, sizes, rel)), device_id_type=MESH)
 
-    def number(rel):
-        return ((rel[0] * 2 + rel[1]) * 2 + rel[2]) * 2 + rel[3]
-
-    def slot(h, rel):
-        group, member = device(moved(here, sizes, rel))
-        return x_ref.at[pl.ds(pl.multiple_of(group * rows + h * half, half), half),
+    inner = (z + z // 2) % 2
+    is_inner, is_outer = inner == 1, inner == 0
+    planes = tuple(flip(z, s) for s in range(nz))
+    pair, across = planes[1], planes[3]
+    cuts = cuts_of(rows)
+
+    def number(s, e, f, g):
+        return ((s * 2 + e) * 2 + f) * 2 + g
+
+    def slot(k, s, e, f, g):
+        group = planes[s] * 2 + flip(x, e)
+        member = flip(y, f) * 2 + flip(c, g)
+        start, size = cuts[k]
+        return x_ref.at[pl.ds(pl.multiple_of(group * rows + start, 16), size),
                         pl.ds(pl.multiple_of(member * cols, cols), cols)]
 
     own = pltpu.make_async_copy(
@@ -90,96 +98,195 @@
     own.wait()
     pl.semaphore_wait(sem, len(greeted))
 
-    sends = []
-
-    def push(src, dst, recv, step):
+    sends, relays = [], []
+
+    def push(src, dst, recv, at, kept=sends):
         copy = pltpu.make_async_remote_copy(
-            src_ref=src, dst_ref=dst, send_sem=send_sem.at[len(sends)], recv_sem=recv,
-            device_id=device(moved(here, sizes, step)), device_id_type=MESH)
+            src_ref=src, dst_ref=dst, send_sem=send_sem.at[len(sends) + len(relays)], recv_sem=recv,
+            device_id=device(at), device_id_type=MESH)
         copy.start()
-        sends.append(copy)
+        kept.append(copy if kept is sends else (len(sends) + len(relays), src.shape))
 
     def arrive(ref, recv):
         pltpu.make_async_copy(ref, ref, recv).wait()
 
-    def send(h, rel, step):
-        lands = tuple(r ^ s for r, s in zip(rel, step))
-        push(slot(h, rel), slot(h, rel), x_recv.at[h, number(lands)], step)
-
-    def landed(h, rel):
-        arrive(slot(h, rel), x_recv.at[h, number(rel)])
-
-    first = {0: axis[0], 1: axis[1]}
-    second = {0: axis[1], 1: axis[0]}
-
-    def pass_on(d, h):
-        if d:
-            landed(h, (d, 0, 0, 0))
-        send(h, (d, 0, 0, 0), first[h])
-        send(h, (d, 0, 0, 0), second[h])
-        send(h, (d, 0, 0, 0), other)
-
-    def pass_second(d):
-        for h in range(2):
-            rel = (d,) + first[h][1:]
-            landed(h, rel)
-            send(h, rel, second[h])
-            send(h, rel, other)
-
-    def pass_last(d):
-        for h in range(2):
-            for rel in ((d,) + second[h][1:], (d, 1, 1, 0)):
-                landed(h, rel)
-                send(h, rel, other)
-
-    def whole(d):
-        for h in range(2):
+    def send(k, s, e, f, step):
+        push(slot(k, s, e, f, 0), slot(k, s, e, f, 0),
+             x_recv.at[k, number(s, e ^ step[1], f ^ step[2], step[3])], moved(here, sizes, step))
+
+    def send_z(k, s, e, f, to, lands, kept=sends):
+        push(slot(k, s, e, f, 0), slot(k, s, e, f, 0), x_recv.at[k, number(lands, e, f, 0)], (to, x, y, c), kept)
+
+    def landed(k, s, e, f, g=0):
+        arrive(slot(k, s, e, f, g), x_recv.at[k, number(s, e, f, g)])
+
+    def route(s):
+        return ((s % 2, axis[0], axis[1]), (1 - s % 2, axis[1], axis[0]))
+
+    def start_z():
+        for k in range(2):
+            send_z(k, 0, 0, 0, pair, 1)
+
+        @pl.when(is_inner)
+        def _():
+            for k in range(2):
+                send_z(k, 0, 0, 0, across, 3, relays)
+
+    def start_late():
+        if len(cuts) > 2:
+            send(2, 0, 0, 0, axis[0])
+            send(2, 0, 0, 0, axis[1])
+            send(2, 0, 0, 0, other)
+
+    def late_second():
+        if len(cuts) > 2:
+            landed(2, 0, 1, 0)
+            send(2, 0, 1, 0, axis[1])
+            send(2, 0, 1, 0, other)
+
+    def late_z():
+        if len(cuts) > 2:
+            for e, f in ((0, 1), (1, 1)):
+                landed(2, 0, e, f)
+                send(2, 0, e, f, other)
             for e in range(2):
                 for f in range(2):
-                    landed(h, (d, e, f, 1))
+                    send_z(2, 0, e, f, pair, 1)
+
+            @pl.when(is_inner)
+            def _():
+                for e in range(2):
+                    for f in range(2):
+                        send_z(2, 0, e, f, across, 3, relays)
+
+    hops = {1: (across, 2), 2: (pair, 3), 3: (pair, 2)}
+
+    def relay(s):
+        @pl.when(is_inner)
+        def _():
+            for k in range(2):
+                landed(k, s, 0, 0)
+                send_z(k, s, 0, 0, *hops[s], relays)
+
+    def meet(s):
+        @pl.when(is_outer)
+        def _():
+            for k in range(2):
+                landed(k, s, 0, 0)
+
+    def late_relay(s):
+        if len(cuts) > 2:
+            @pl.when(is_inner)
+            def _():
+                for e in range(2):
+                    for f in range(2):
+                        landed(2, s, e, f)
+                        send_z(2, s, e, f, *hops[s], relays)
+
+    def late_meet(s):
+        if len(cuts) > 2:
+            @pl.when(is_outer)
+            def _():
+                for e in range(2):
+                    for f in range(2):
+                        landed(2, s, e, f)
+
+            for e in range(2):
+                for f in range(2):
+                    send(2, s, e, f, other)
+
+    def pass_on(s):
+        for k, first, second in route(s):
+            send(k, s, 0, 0, first)
+        for k, first, second in route(s):
+            send(k, s, 0, 0, second)
+        for k in range(2):
+            send(k, s, 0, 0, other)
+
+    def pass_second(s):
+        for k, first, second in route(s):
+            e, f = first[1], first[2]
+            landed(k, s, e, f)
+            send(k, s, e, f, second)
+            send(k, s, e, f, other)
+
+    def pass_last(s):
+        for k, first, second in route(s):
+            for e, f in (second[1:3], (1, 1)):
+                landed(k, s, e, f)
+                send(k, s, e, f, other)
+
+    def whole(s):
+        for k in range(len(cuts)):
+            for e in range(2):
+                for f in range(2):
+                    landed(k, s, e, f, 1)
 
     eye = lax.broadcasted_iota(jnp.int32, (rows, rows), 0) == lax.broadcasted_iota(jnp.int32, (rows, rows), 1)
 
-    def hidden(d, e):
-        group = flip(z, d) * 2 + flip(x, e)
+    def spread(s):
+        for e in range(2):
+            for m in range(members):
+                line = share_ref[planes[s] * 2 + flip(x, e), pl.ds(me * members + m, 1), :]
+                scale = jnp.sum(jnp.where(eye, jnp.broadcast_to(line, (rows, rows)), 0.0), axis=1, keepdims=True)
+                scale_ref[s, e, m] = jnp.broadcast_to(scale, (rows, rows))
+
+    def hidden(s, e):
+        group = planes[s] * 2 + flip(x, e)
         block = x_ref[pl.ds(pl.multiple_of(group * rows, rows), rows), :]
-
-        @pl.loop(0, members)
-        def _(m):
-            line = share_ref[group, pl.ds(me * members + m, 1), :]
-            scale = jnp.sum(jnp.where(eye, jnp.broadcast_to(line, (rows, rows)), 0.0), axis=1, keepdims=True)
+        for m in range(members):
             both = jnp.dot(block, w_ref[m], preferred_element_type=jnp.float32)
             gate, up = both[:, :units], both[:, units:]
-            hid_ref[d, e * rows:(e + 1) * rows, pl.ds(pl.multiple_of(m * units, 128), units)] = (
+            scale = jnp.concatenate([scale_ref[s, e, m]] * (units // rows), axis=1)
+            hid_ref[s, e * rows:(e + 1) * rows, m * units:(m + 1) * units] = (
                 jax.nn.silu(gate) * up * scale).astype(hid_ref.dtype)
 
-    def down(d, g):
-        @pl.loop(0, 2)
+    def down(s, g):
+        @pl.loop(0, 2, unroll=True)
         def _(f):
             member = (y + f - 2 * y * f) * 2 + flip(c, g)
             at = pl.ds(pl.multiple_of(member * cols, cols), cols)
-            part_ref[d, f, g] = jnp.dot(
-                hid_ref[d], down_ref[:, at], preferred_element_type=jnp.float32).astype(part_ref.dtype)
-
-    def rel_of(h, a, b):
-        return (b, a) if h == 0 else (a, b)
-
-    def local(h, a, b, d, g):
-        e, f = rel_of(h, a, b)
-        return part_ref.at[d, f, g, pl.ds(e * rows + h * half, half), :]
-
-    out_first = {0: axis[1], 1: axis[0]}
-    out_second = {0: axis[0], 1: axis[1]}
-
-    def swap(d):
+            part_ref[s, f, g] = jnp.dot(
+                hid_ref[s], down_ref[:, at], preferred_element_type=jnp.float32).astype(part_ref.dtype)
+
+    spans = spans_of(rows)
+    tail = rows - spans[1][0] - spans[1][1]
+
+    def x_first(h, s):
+        return (h + s) % 2 == 1
+
+    def local(h, a, b, s, g):
+        e, f = (a, b) if x_first(h, s) else (b, a)
+        return part_ref.at[s, f, g, pl.ds(e * rows + spans[h][0], spans[h][1]), :]
+
+    def local_late(e, f, s, g):
+        return part_ref.at[s, f, g, pl.ds((e + 1) * rows - tail, tail), :]
+
+    def piece_c(h, a, b, s):
+        return buf_c.at[h, a, b, s, pl.ds(0, spans[h][1]), :]
+
+    def piece_1(h, b, s):
+        return buf_1.at[h, b, s, pl.ds(0, spans[h][1]), :]
+
+    def piece_2(h, s):
+        return buf_2.at[h, s, pl.ds(0, spans[h][1]), :]
+
+    def piece_z(h, k):
+        return buf_z.at[h, k, pl.ds(0, spans[h][1]), :]
+
+    def swap(s):
+        there = moved(here, sizes, other)
         for a, b in ((1, 1), (1, 0), (0, 1), (0, 0)):
             for h in range(2):
-                push(local(h, a, b, d, 1), buf_c.at[h, a, b, d], recv_c.at[h, a, b, d], other)
+                push(local(h, a, b, s, 1), piece_c(h, a, b, s), recv_c.at[h, a, b, s], there)
+        for e in range(2):
+            for f in range(2):
+                push(local_late(e, f, s, 1), late_c.at[s, e, f], recv_lc.at[s, e, f], there)
 
     def add(dst, *srcs):
         chunk = 16
 
-        @pl.loop(0, half // chunk)
+        @pl.loop(0, dst.shape[0] // chunk)
         def _(i):
             at = pl.ds(pl.multiple_of(i * chunk, chunk), chunk)
             total = srcs[0][at, :].astype(jnp.float32)
@@ -187,106 +294,199 @@
                 total = total + src[at, :].astype(jnp.float32)
             dst[at, :] = total.astype(dst.dtype)
 
-    def step_first(d):
+    def step_first(s, b):
+        for h in range(2):
+            piece = piece_c(h, 1, b, s)
+            arrive(piece, recv_c.at[h, 1, b, s])
+            add(piece, piece, local(h, 1, b, s, 0))
+            push(piece, piece_1(h, b, s), recv_1.at[h, b, s], moved(here, sizes, axis[1 - x_first(h, s)]))
+
+    def step_second(s):
+        for h in range(2):
+            piece = piece_c(h, 0, 1, s)
+            arrive(piece, recv_c.at[h, 0, 1, s])
+            arrive(piece_1(h, 1, s), recv_1.at[h, 1, s])
+            add(piece, piece, local(h, 0, 1, s, 0), piece_1(h, 1, s))
+            push(piece, piece_2(h, s), recv_2.at[h, s], moved(here, sizes, axis[int(x_first(h, s))]))
+
+    def step_last(s):
+        for h in range(2):
+            piece = piece_c(h, 0, 0, s)
+            arrive(piece, recv_c.at[h, 0, 0, s])
+            arrive(piece_1(h, 0, s), recv_1.at[h, 0, s])
+            arrive(piece_2(h, s), recv_2.at[h, s])
+            srcs = (piece, local(h, 0, 0, s, 0), piece_1(h, 0, s), piece_2(h, s))
+            for k in {0: (0, 2), 3: (1,)}.get(s, ()):
+                arrive(piece_z(h, k), recv_z.at[h, k])
+                srcs += (piece_z(h, k),)
+            if s:
+                add(piece, *srcs)
+                push(piece, piece_z(h, s - 1), recv_z.at[h, s - 1], (across if s == 3 else pair, x, y, c))
+            else:
+                add(out_ref.at[pl.ds(*spans[h]), :], *srcs)
+
+    def late_out(s):
+        for e in range(2):
+            for f in range(2):
+                piece = late_c.at[s, e, f]
+                arrive(piece, recv_lc.at[s, e, f])
+                srcs = (piece, local_late(e, f, s, 0))
+                for k in {0: (0, 2), 3: (1,)}.get(s, ()):
+                    arrive(late_zs.at[k, e, f], recv_lz.at[k, e, f])
+                    srcs += (late_zs.at[k, e, f],)
+                add(piece, *srcs)
+                if s:
+                    push(piece, late_zs.at[s - 1, e, f], recv_lz.at[s - 1, e, f],
+                         (across if s == 3 else pair, x, y, c))
+
+    ways = [(i, pl.ds(i * 16, 16)) for i in range(tail // 16)]
+
+    def late_piece(i, a, b, at):
+        e, f = (b, a) if i else (a, b)
+        return late_c.at[0, e, f, at, :]
+
+    def late_first():
         for b in (1, 0):
-            for h in range(2):
-                piece = buf_c.at[h, 1, b, d]
-                arrive(piece, recv_c.at[h, 1, b, d])
-                add(piece, piece, local(h, 1, b, d, 0))
-                push(piece, buf_1.at[h, b, d], recv_1.at[h, b, d], out_first[h])
-
-    def step_second(d):
-        for h in range(2):
-            piece = buf_c.at[h, 0, 1, d]
-            arrive(piece, recv_c.at[h, 0, 1, d])
-            arrive(buf_1.at[h, 1, d], recv_1.at[h, 1, d])
-            add(piece, piece, local(h, 0, 1, d, 0), buf_1.at[h, 1, d])
-            push(piece, buf_2.at[h, d], recv_2.at[h, d], out_second[h])
-
-    def step_last(d):
-        for h in range(2):
-            piece = buf_c.at[h, 0, 0, d]
-            arrive(piece, recv_c.at[h, 0, 0, d])
-            arrive(buf_1.at[h, 0, d], recv_1.at[h, 0, d])
-            arrive(buf_2.at[h, d], recv_2.at[h, d])
-            srcs = (piece, local(h, 0, 0, d, 0), buf_1.at[h, 0, d], buf_2.at[h, d])
-            if d:
-                add(piece, *srcs)
-                push(piece, buf_z.at[h, d - 1], recv_z.at[h, d - 1], (d, 0, 0, 0))
-            else:
-                for k in range(nz - 1):
-                    arrive(buf_z.at[h, k], recv_z.at[h, k])
-                add(out_ref.at[pl.ds(h * half, half), :], *srcs, *[buf_z.at[h, k] for k in range(nz - 1)])
-
-    def send_far(d):
-        for h in range(2):
-            send(h, (0, 0, 0, 0), (d, 0, 0, 0))
-
-    send_far(1)
-    for h in range(2):
-        pass_on(0, h)
-    for i, rel in enumerate(ep_rels):
-        push(own_share, share_ref.at[me], share_recv.at[i], rel)
+            for i, at in ways:
+                push(late_piece(i, 1, b, at), late_1.at[i, b], recv_l1.at[i, b], moved(here, sizes, axis[i]))
+
+    def late_next():
+        for i, at in ways:
+            piece = late_piece(i, 0, 1, at)
+            arrive(late_1.at[i, 1], recv_l1.at[i, 1])
+            add(piece, piece, late_1.at[i, 1])
+            push(piece, late_2.at[i], recv_l2.at[i], moved(here, sizes, axis[1 - i]))
+
+    def late_last():
+        for i, at in ways:
+            arrive(late_1.at[i, 0], recv_l1.at[i, 0])
+            arrive(late_2.at[i], recv_l2.at[i])
+            add(out_ref.at[pl.ds(rows - tail + i * 16, 16), :], late_piece(i, 0, 0, at), late_1.at[i, 0], late_2.at[i])
+
     keep = pltpu.make_async_copy(own_share, share_ref.at[me], load_sem.at[3 + 3 * members])
-    keep.start()
-    for d in range(2, nz):
-        send_far(d)
+
+    def send_shares():
+        for i, rel in enumerate(ep_rels):
+            push(own_share, share_ref.at[me], share_recv.at[i], moved(here, sizes, rel))
+        keep.start()
+
+    def wait_loads():
+        for load in loads:
+            load.wait()
+        keep.wait()
+        for i in range(len(ep_rels)):
+            arrive(share_ref.at[0], share_recv.at[i])
+        for s in range(nz):
+            spread(s)
+
+    start_z()
+    start_late()
+    pass_on(0)
+    send_shares()
+    late_second()
     pass_second(0)
-    for h in range(2):
-        pass_on(1, h)
+    relay(1)
+    meet(1)
+    pass_on(1)
+    relay(3)
+    late_z()
+    wait_loads()
     pass_last(0)
-    for load in loads:
-        load.wait()
-    keep.wait()
-    for i in range(len(ep_rels)):
-        arrive(share_ref.at[0], share_recv.at[i])
-
-    last = nz - 1
-    for d in range(nz):
-        whole(d)
-        hidden(d, 0)
-        if d < last:
-            pass_second(d + 1)
-        elif last > 2:
-            step_second(last - 1)
-        hidden(d, 1)
-        if d + 2 < nz:
-            for h in range(2):
-                pass_on(d + 2, h)
-        if d >= 2:
-            down(d, 1)
-            swap(d)
-            down(d, 0)
-            step_first(d)
-        if d < last:
-            pass_last(d + 1)
-    step_last(last - 1)
+    relay(2)
+    meet(2)
+    pass_on(2)
+    pass_second(1)
+    whole(0)
+    hidden(0, 0)
+    late_relay(1)
+    late_relay(3)
+    meet(3)
+    pass_on(3)
+    hidden(0, 1)
+    pass_second(2)
+    late_meet(1)
+    pass_last(1)
+    whole(1)
+    hidden(1, 0)
+    late_relay(2)
+    hidden(1, 1)
+    pass_second(3)
     down(1, 1)
     swap(1)
     down(1, 0)
-    step_second(last)
-    step_first(1)
+    late_meet(2)
+    pass_last(2)
+    step_first(1, 1)
+    late_out(1)
+    whole(2)
+    hidden(2, 0)
+    hidden(2, 1)
+    late_meet(3)
+    pass_last(3)
+    step_first(1, 0)
+    down(2, 1)
+    swap(2)
+    down(2, 0)
+    whole(3)
+    step_first(2, 1)
+    step_first(2, 0)
+    hidden(3, 0)
+    late_out(2)
+    hidden(3, 1)
+    down(3, 1)
+    swap(3)
+    step_second(2)
+    down(3, 0)
+    step_first(3, 1)
+    step_first(3, 0)
+    step_last(2)
+    late_out(3)
     down(0, 1)
     swap(0)
     down(0, 0)
-    step_last(last)
+    step_second(3)
     step_second(1)
-    step_first(0)
+    step_first(0, 1)
+    step_first(0, 0)
+    step_last(3)
     step_last(1)
     step_second(0)
+    late_out(0)
+    late_first()
+    late_next()
     step_last(0)
+    late_last()
     for copy in sends:
         copy.wait_send()
+
+    @pl.when(is_inner)
+    def _():
+        for at, (size, span) in relays:
+            done = x_ref.at[pl.ds(0, size), pl.ds(0, span)]
+            pltpu.make_async_copy(done, done, send_sem.at[at]).wait()
+
+
+def cuts_of(rows):
+    late = 16
+    most = 64
+    return [(0, most), (most, rows - late - most)] + ([(rows - late, late)] if late else [])
+
+
+def spans_of(rows):
+    late = 16
+    most = (rows - late + 16) // 32 * 16
+    return [(0, most), (most, rows - late - most)]
 
 
 def layer_scratch(sizes, x, ids, prob, gate, down):
     nz = sizes[0]
     groups, parts = nz * sizes[1], sizes[2] * sizes[3]
     rows, cols = x.shape
-    half = rows // 2
+    spans = spans_of(rows)
+    half, tail = spans[0][1], rows - spans[1][0] - spans[1][1]
     members, width, units = gate.shape
     experts = groups * members
-    n_send = 2 * (nz - 1 + 7 * nz) + groups - 1 + 2 * (4 * nz + 2 * nz + nz + nz - 1)
+    n_send = 32 * nz + 24 * nz + groups - 1 + 2 * (4 * nz + 2 * nz + nz + nz - 1) + 8 * nz + 8
     buffers = [
         pltpu.VMEM((groups * rows, parts * cols), x.dtype),
         pltpu.VMEM(ids.shape, ids.dtype),
@@ -301,16 +501,25 @@
         pltpu.VMEM((2, 2, nz, half, cols), x.dtype),
         pltpu.VMEM((2, nz, half, cols), x.dtype),
         pltpu.VMEM((2, nz - 1, half, cols), x.dtype),
+        pltpu.VMEM((nz, 2, 2, tail, cols), x.dtype),
+        pltpu.VMEM((nz - 1, 2, 2, tail, cols), x.dtype),
+        pltpu.VMEM((tail // 16, 2, 16, cols), x.dtype),
+        pltpu.VMEM((tail // 16, 16, cols), x.dtype),
+        pltpu.VMEM((nz, 2, members, rows, rows), jnp.float32),
     ]
     semaphores = [
         pltpu.SemaphoreType.DMA((4 + 3 * members,)),
         pltpu.SemaphoreType.DMA((n_send,)),
-        pltpu.SemaphoreType.DMA((2, groups * parts)),
+        pltpu.SemaphoreType.DMA((3, groups * parts)),
         pltpu.SemaphoreType.DMA((groups - 1,)),
         pltpu.SemaphoreType.DMA((2, 2, 2, nz)),
         pltpu.SemaphoreType.DMA((2, 2, nz)),
         pltpu.SemaphoreType.DMA((2, nz)),
         pltpu.SemaphoreType.DMA((2, nz - 1)),
+        pltpu.SemaphoreType.DMA((nz, 2, 2)),
+        pltpu.SemaphoreType.DMA((nz - 1, 2, 2)),
+        pltpu.SemaphoreType.DMA((tail // 16, 2)),
+        pltpu.SemaphoreType.DMA((tail // 16,)),
     ]
     return buffers, semaphores
 
@@ -389,7 +598,7 @@
     members = gate_weight.shape[0]
     sizes = (groups // 2, 2, parts // 2, 2)
     rows = tokens.shape[0]
-    square = groups > 4 and groups & (groups - 1) == 0 and parts == 4 and members * groups <= rows == 128
+    square = groups == 8 and parts == 4 and members * groups <= rows == 128
     if square:
         ids, prob = jnp.transpose(expert_ids), jnp.transpose(gate_prob)
         buffers = layer_scratch(sizes, tokens, ids, prob, gate_weight, down_weight)[0]

time: 90 us -> 85 us (0.944)
  Pallas kernels: 88.2 us -> 83.1 us
    pallas_call x1, Pallas kernels: 88.2 us -> 83.1 us  [layer(): pl.pallas_call(functools.partial(layer_kernel, sizes), out_shape=jax.Shap...]
where the time goes in v2:
time: 85 us; the launch traced here: 84.8 us
  Pallas kernels  83.1 us (98%)
  local copies, waits for them, and re-layouts  1.67 us (2%)
    pallas_call x1, Pallas kernels, layer(): pl.pallas_call(functools.partial(layer_kernel, sizes), out_shape=jax.Shap...  83.1 us

profile of v2, /device:TPU:0, one launch (start us, length us, event | category | flops | bytes accessed | tf_op | source)
XLA Modules:
  0.0 84.8 jit_solution(1860986128228090036)
XLA Ops:
  0.0 83.1 %layer.1 = bf16[128,1024]{1,0:T(8,128)(2,1)} custom-call(bf16[128,1024]{1,0:T(8,128)(2,1)} %x_hbm.1, s32[8,128]{1,0:T(8,128)} %bitcast.2, f32[8,128]{1,0:T(8,128)} %bitcast.3, bf16[2,4096,384]{2,1,0:T(8,128)(2,1)} %gate_hbm.1, bf16[2,4096,384]{2,1,0:T(8,128)(2,1)} %up_hbm.1, bf16[2,384,4096]{2,1,0:T(8,128)(2,1)} %down_hbm.1), custom_call_target="tpu_custom_call" | custom-call | tf_op jit(solution)/shard_map/layer/pallas_call | solution.py:529
  83.2 1.7 %copy.8 = bf16[128,1024]{1,0:T(8,128)(2,1)} copy(bf16[128,1024]{1,0:T(8,128)(2,1)} %layer.1) | data formatting | bytes 524288

commit v3 on v2

--- a/solution.py
+++ b/solution.py
@@ -38,7 +38,7 @@
 def layer_kernel(sizes, x_hbm, ids_hbm, prob_hbm, gate_hbm, up_hbm, down_hbm, out_ref,
                  x_ref, ids_ref, prob_ref, own_share, share_ref, w_ref, down_ref, hid_ref, part_ref,
                  buf_c, buf_1, buf_2, buf_z, late_c, late_zs, late_1, late_2, scale_ref,
-                 load_sem, send_sem, x_recv, share_recv, recv_c, recv_1, recv_2, recv_z,
+                 load_sem, send_sem, x_recv, z_recv, core_recv, late_recv, share_recv, recv_c, recv_1, recv_2, recv_z,
                  recv_lc, recv_lz, recv_l1, recv_l2):
     nz = sizes[0]
     rows, cols = x_hbm.shape
@@ -61,9 +61,10 @@
     planes = tuple(flip(z, s) for s in range(nz))
     pair, across = planes[1], planes[3]
     cuts = cuts_of(rows)
-
-    def number(s, e, f, g):
-        return ((s * 2 + e) * 2 + f) * 2 + g
+    strips = strips_of(cuts)
+
+    def number(s, e, f):
+        return s * 3 + e * 2 + f - 1
 
     def slot(k, s, e, f, g):
         group = planes[s] * 2 + flip(x, e)
@@ -98,39 +99,55 @@
     own.wait()
     pl.semaphore_wait(sem, len(greeted))
 
-    sends, relays = [], []
+    sends, relays, lines = [0], [], []
 
     def push(src, dst, recv, at, kept=sends):
-        copy = pltpu.make_async_remote_copy(
-            src_ref=src, dst_ref=dst, send_sem=send_sem.at[len(sends) + len(relays)], recv_sem=recv,
-            device_id=device(at), device_id_type=MESH)
-        copy.start()
-        kept.append(copy if kept is sends else (len(sends) + len(relays), src.shape))
+        if kept is sends and sends[-1] + src.shape[0] > 1024:
+            sends.append(0)
+        kept.append(src.shape[0]) if kept is relays else kept.__setitem__(-1, kept[-1] + src.shape[0])
+        pltpu.make_async_remote_copy(
+            src_ref=src, dst_ref=dst, send_sem=send_sem.at[1 + len(sends) if kept is sends else 0], recv_sem=recv,
+            device_id=device(at), device_id_type=MESH).start()
+
+    def arrive_rows(count, recv):
+        ref = x_ref.at[pl.ds(0, count), pl.ds(0, cols)]
+        pltpu.make_async_copy(ref, ref, recv).wait()
 
     def arrive(ref, recv):
         pltpu.make_async_copy(ref, ref, recv).wait()
 
     def send(k, s, e, f, step):
         push(slot(k, s, e, f, 0), slot(k, s, e, f, 0),
-             x_recv.at[k, number(s, e ^ step[1], f ^ step[2], step[3])], moved(here, sizes, step))
+             core_recv.at[s] if step[3] else x_recv.at[k, number(s, e ^ step[1], f ^ step[2])], moved(here, sizes, step))
 
     def send_z(k, s, e, f, to, lands, kept=sends):
-        push(slot(k, s, e, f, 0), slot(k, s, e, f, 0), x_recv.at[k, number(lands, e, f, 0)], (to, x, y, c), kept)
-
-    def landed(k, s, e, f, g=0):
-        arrive(slot(k, s, e, f, g), x_recv.at[k, number(s, e, f, g)])
+        push(slot(k, s, e, f, 0), slot(k, s, e, f, 0), late_recv.at[lands], (to, x, y, c), kept)
+
+    def strip(i, s):
+        start, size = strips[i]
+        return x_ref.at[pl.ds(pl.multiple_of((planes[s] * 2 + x) * rows + start, 16), size),
+                        pl.ds(pl.multiple_of(device(here)[1] * cols, cols), cols)]
+
+    def send_strip(i, s, to, lands, kept=sends):
+        push(strip(i, s), strip(i, s), z_recv.at[i, lands], (to, x, y, c), kept)
+
+    def strip_landed(i, s):
+        arrive(strip(i, s), z_recv.at[i, s])
+
+    def landed(k, s, e, f):
+        arrive(slot(k, s, e, f, 0), x_recv.at[k, number(s, e, f)])
 
     def route(s):
         return ((s % 2, axis[0], axis[1]), (1 - s % 2, axis[1], axis[0]))
 
     def start_z():
-        for k in range(2):
-            send_z(k, 0, 0, 0, pair, 1)
+        for i in range(len(strips)):
+            send_strip(i, 0, pair, 1)
 
         @pl.when(is_inner)
         def _():
-            for k in range(2):
-                send_z(k, 0, 0, 0, across, 3, relays)
+            for i in range(len(strips)):
+                send_strip(i, 0, across, 3, relays)
 
     def start_late():
         if len(cuts) > 2:
@@ -161,35 +178,33 @@
 
     hops = {1: (across, 2), 2: (pair, 3), 3: (pair, 2)}
 
-    def relay(s):
+    def relay(i, *which):
         @pl.when(is_inner)
         def _():
-            for k in range(2):
-                landed(k, s, 0, 0)
-                send_z(k, s, 0, 0, *hops[s], relays)
+            for s in which:
+                strip_landed(i, s)
+                send_strip(i, s, *hops[s], relays)
 
     def meet(s):
         @pl.when(is_outer)
         def _():
-            for k in range(2):
-                landed(k, s, 0, 0)
+            for i in range(len(strips)):
+                strip_landed(i, s)
 
     def late_relay(s):
         if len(cuts) > 2:
             @pl.when(is_inner)
             def _():
+                arrive_rows(4 * cuts[2][1], late_recv.at[s])
                 for e in range(2):
                     for f in range(2):
-                        landed(2, s, e, f)
                         send_z(2, s, e, f, *hops[s], relays)
 
     def late_meet(s):
         if len(cuts) > 2:
             @pl.when(is_outer)
             def _():
-                for e in range(2):
-                    for f in range(2):
-                        landed(2, s, e, f)
+                arrive_rows(4 * cuts[2][1], late_recv.at[s])
 
             for e in range(2):
                 for f in range(2):
@@ -203,8 +218,10 @@
         for k in range(2):
             send(k, s, 0, 0, other)
 
-    def pass_second(s):
+    def pass_second(s, ks=(0, 1)):
         for k, first, second in route(s):
+            if k not in ks:
+                continue
             e, f = first[1], first[2]
             landed(k, s, e, f)
             send(k, s, e, f, second)
@@ -217,10 +234,7 @@
                 send(k, s, e, f, other)
 
     def whole(s):
-        for k in range(len(cuts)):
-            for e in range(2):
-                for f in range(2):
-                    landed(k, s, e, f, 1)
+        arrive_rows(4 * rows, core_recv.at[s])
 
     eye = lax.broadcasted_iota(jnp.int32, (rows, rows), 0) == lax.broadcasted_iota(jnp.int32, (rows, rows), 1)
 
@@ -241,13 +255,15 @@
             hid_ref[s, e * rows:(e + 1) * rows, m * units:(m + 1) * units] = (
                 jax.nn.silu(gate) * up * scale).astype(hid_ref.dtype)
 
-    def down(s, g):
+    def down(s, g, es=(0, 1)):
+        at_rows = pl.ds(es[0] * rows, len(es) * rows)
+
         @pl.loop(0, 2, unroll=True)
         def _(f):
             member = (y + f - 2 * y * f) * 2 + flip(c, g)
             at = pl.ds(pl.multiple_of(member * cols, cols), cols)
-            part_ref[s, f, g] = jnp.dot(
-                hid_ref[s], down_ref[:, at], preferred_element_type=jnp.float32).astype(part_ref.dtype)
+            part_ref[s, f, g, at_rows, :] = jnp.dot(
+                hid_ref[s, at_rows, :], down_ref[:, at], preferred_element_type=jnp.float32).astype(part_ref.dtype)
 
     spans = spans_of(rows)
     tail = rows - spans[1][0] - spans[1][1]
@@ -274,14 +290,15 @@
     def piece_z(h, k):
         return buf_z.at[h, k, pl.ds(0, spans[h][1]), :]
 
-    def swap(s):
+    def swap(s, es=(0, 1)):
         there = moved(here, sizes, other)
         for a, b in ((1, 1), (1, 0), (0, 1), (0, 0)):
             for h in range(2):
-                push(local(h, a, b, s, 1), piece_c(h, a, b, s), recv_c.at[h, a, b, s], there)
-        for e in range(2):
+                if (a if x_first(h, s) else b) in es:
+                    push(local(h, a, b, s, 1), piece_c(h, a, b, s), recv_c.at[a, b, s], there)
+        for e in es:
             for f in range(2):
-                push(local_late(e, f, s, 1), late_c.at[s, e, f], recv_lc.at[s, e, f], there)
+                push(local_late(e, f, s, 1), late_c.at[s, e, f], recv_lc.at[s], there)
 
     def add(dst, *srcs):
         chunk = 16
@@ -295,24 +312,24 @@
             dst[at, :] = total.astype(dst.dtype)
 
     def step_first(s, b):
+        arrive_rows(rows - tail, recv_c.at[1, b, s])
         for h in range(2):
             piece = piece_c(h, 1, b, s)
-            arrive(piece, recv_c.at[h, 1, b, s])
             add(piece, piece, local(h, 1, b, s, 0))
             push(piece, piece_1(h, b, s), recv_1.at[h, b, s], moved(here, sizes, axis[1 - x_first(h, s)]))
 
     def step_second(s):
+        arrive_rows(rows - tail, recv_c.at[0, 1, s])
         for h in range(2):
             piece = piece_c(h, 0, 1, s)
-            arrive(piece, recv_c.at[h, 0, 1, s])
             arrive(piece_1(h, 1, s), recv_1.at[h, 1, s])
             add(piece, piece, local(h, 0, 1, s, 0), piece_1(h, 1, s))
             push(piece, piece_2(h, s), recv_2.at[h, s], moved(here, sizes, axis[int(x_first(h, s))]))
 
     def step_last(s):
+        arrive_rows(rows - tail, recv_c.at[0, 0, s])
         for h in range(2):
             piece = piece_c(h, 0, 0, s)
-            arrive(piece, recv_c.at[h, 0, 0, s])
             arrive(piece_1(h, 0, s), recv_1.at[h, 0, s])
             arrive(piece_2(h, s), recv_2.at[h, s])
             srcs = (piece, local(h, 0, 0, s, 0), piece_1(h, 0, s), piece_2(h, s))
@@ -326,18 +343,16 @@
                 add(out_ref.at[pl.ds(*spans[h]), :], *srcs)
 
     def late_out(s):
+        more = {0: (0, 2), 3: (1,)}.get(s, ())
+        arrive_rows(4 * tail, recv_lc.at[s])
+        for k in more:
+            arrive_rows(4 * tail, recv_lz.at[k])
         for e in range(2):
             for f in range(2):
                 piece = late_c.at[s, e, f]
-                arrive(piece, recv_lc.at[s, e, f])
-                srcs = (piece, local_late(e, f, s, 0))
-                for k in {0: (0, 2), 3: (1,)}.get(s, ()):
-                    arrive(late_zs.at[k, e, f], recv_lz.at[k, e, f])
-                    srcs += (late_zs.at[k, e, f],)
-                add(piece, *srcs)
+                add(piece, piece, local_late(e, f, s, 0), *[late_zs.at[k, e, f] for k in more])
                 if s:
-                    push(piece, late_zs.at[s - 1, e, f], recv_lz.at[s - 1, e, f],
-                         (across if s == 3 else pair, x, y, c))
+                    push(piece, late_zs.at[s - 1, e, f], recv_lz.at[s - 1], (across if s == 3 else pair, x, y, c))
 
     ways = [(i, pl.ds(i * 16, 16)) for i in range(tail // 16)]
 
@@ -366,16 +381,18 @@
     keep = pltpu.make_async_copy(own_share, share_ref.at[me], load_sem.at[3 + 3 * members])
 
     def send_shares():
-        for i, rel in enumerate(ep_rels):
-            push(own_share, share_ref.at[me], share_recv.at[i], moved(here, sizes, rel))
+        for rel in ep_rels:
+            pltpu.make_async_remote_copy(
+                src_ref=own_share, dst_ref=share_ref.at[me], send_sem=send_sem.at[1], recv_sem=share_recv,
+                device_id=device(moved(here, sizes, rel)), device_id_type=MESH).start()
         keep.start()
 
     def wait_loads():
         for load in loads:
             load.wait()
         keep.wait()
-        for i in range(len(ep_rels)):
-            arrive(share_ref.at[0], share_recv.at[i])
+        others = share_ref.at[pl.ds(0, len(ep_rels))]
+        pltpu.make_async_copy(others, others, share_recv).wait()
         for s in range(nz):
             spread(s)
 
@@ -384,92 +401,103 @@
     pass_on(0)
     send_shares()
     late_second()
+    relay(0, 1, 3)
+    relay(1, 1, 3)
     pass_second(0)
-    relay(1)
+    relay(2, 1, 3)
     meet(1)
     pass_on(1)
-    relay(3)
+    relay(0, 2)
+    wait_loads()
+    relay(1, 2)
+    relay(2, 2)
     late_z()
-    wait_loads()
     pass_last(0)
-    relay(2)
     meet(2)
     pass_on(2)
     pass_second(1)
     whole(0)
     hidden(0, 0)
+    hidden(0, 1)
+    pass_second(2)
+    meet(3)
+    pass_on(3)
     late_relay(1)
     late_relay(3)
-    meet(3)
-    pass_on(3)
-    hidden(0, 1)
-    pass_second(2)
+    down(0, 1)
+    swap(0)
+    down(0, 0)
     late_meet(1)
     pass_last(1)
     whole(1)
     hidden(1, 0)
     late_relay(2)
+    late_meet(2)
+    pass_last(2)
     hidden(1, 1)
     pass_second(3)
     down(1, 1)
     swap(1)
     down(1, 0)
-    late_meet(2)
-    pass_last(2)
     step_first(1, 1)
-    late_out(1)
     whole(2)
+    hidden(2, 1)
+    step_first(1, 0)
     hidden(2, 0)
-    hidden(2, 1)
     late_meet(3)
     pass_last(3)
-    step_first(1, 0)
     down(2, 1)
     swap(2)
+    late_out(1)
     down(2, 0)
-    whole(3)
     step_first(2, 1)
     step_first(2, 0)
+    whole(3)
+    hidden(3, 1)
+    late_out(2)
+    down(3, 1, (1,))
+    swap(3, (1,))
+    down(3, 0, (1,))
     hidden(3, 0)
-    late_out(2)
-    hidden(3, 1)
-    down(3, 1)
-    swap(3)
     step_second(2)
-    down(3, 0)
     step_first(3, 1)
+    down(3, 1, (0,))
+    swap(3, (0,))
+    down(3, 0, (0,))
     step_first(3, 0)
+    late_out(3)
     step_last(2)
-    late_out(3)
-    down(0, 1)
-    swap(0)
-    down(0, 0)
     step_second(3)
     step_second(1)
     step_first(0, 1)
     step_first(0, 0)
     step_last(3)
+    late_out(0)
+    late_first()
     step_last(1)
     step_second(0)
-    late_out(0)
-    late_first()
     late_next()
     step_last(0)
     late_last()
-    for copy in sends:
-        copy.wait_send()
+    for i, count in enumerate(sends):
+        arrive_rows(count, send_sem.at[2 + i])
+    gone = share_ref.at[pl.ds(0, len(ep_rels))]
+    pltpu.make_async_copy(gone, gone, send_sem.at[1]).wait()
 
     @pl.when(is_inner)
     def _():
-        for at, (size, span) in relays:
-            done = x_ref.at[pl.ds(0, size), pl.ds(0, span)]
-            pltpu.make_async_copy(done, done, send_sem.at[at]).wait()
+        arrive_rows(sum(relays), send_sem.at[0])
 
 
 def cuts_of(rows):
     late = 16
     most = 64
     return [(0, most), (most, rows - late - most)] + ([(rows - late, late)] if late else [])
+
+
+def strips_of(cuts):
+    (_, a), (start, b) = cuts[:2]
+    return [(0, a // 32 * 16), (a // 32 * 16, a - a // 32 * 16), (start, b)]
 
 
 def spans_of(rows):
@@ -486,7 +514,6 @@
     half, tail = spans[0][1], rows - spans[1][0] - spans[1][1]
     members, width, units = gate.shape
     experts = groups * members
-    n_send = 32 * nz + 24 * nz + groups - 1 + 2 * (4 * nz + 2 * nz + nz + nz - 1) + 8 * nz + 8
     buffers = [
         pltpu.VMEM((groups * rows, parts * cols), x.dtype),
         pltpu.VMEM(ids.shape, ids.dtype),
@@ -507,20 +534,9 @@
         pltpu.VMEM((tail // 16, 16, cols), x.dtype),
         pltpu.VMEM((nz, 2, members, rows, rows), jnp.float32),
     ]
-    semaphores = [
-        pltpu.SemaphoreType.DMA((4 + 3 * members,)),
-        pltpu.SemaphoreType.DMA((n_send,)),
-        pltpu.SemaphoreType.DMA((3, groups * parts)),
-        pltpu.SemaphoreType.DMA((groups - 1,)),
-        pltpu.SemaphoreType.DMA((2, 2, 2, nz)),
-        pltpu.SemaphoreType.DMA((2, 2, nz)),
-        pltpu.SemaphoreType.DMA((2, nz)),
-        pltpu.SemaphoreType.DMA((2, nz - 1)),
-        pltpu.SemaphoreType.DMA((nz, 2, 2)),
-        pltpu.SemaphoreType.DMA((nz - 1, 2, 2)),
-        pltpu.SemaphoreType.DMA((tail // 16, 2)),
-        pltpu.SemaphoreType.DMA((tail // 16,)),
-    ]
+    semaphores = [pltpu.SemaphoreType.DMA(shape) for shape in (
+        (4 + 3 * members,), (12,), (3, 3 * nz), (3, nz), (nz,), (nz,), (), (2, 2, nz), (2, 2, nz), (2, nz), (2, nz - 1),
+        (nz,), (nz - 1,), (tail // 16, 2), (tail // 16,))]
     return buffers, semaphores
 
 

time: 85 us -> 76.3 us (0.90)
  Pallas kernels: 83.1 us -> 74.5 us
    pallas_call x1, Pallas kernels: 83.1 us -> 74.5 us  [layer(): pl.pallas_call(functools.partial(layer_kernel, sizes), out_shape=jax.Shap...]
where the time goes in v3:
time: 76.3 us; the launch traced here: 76.2 us
  Pallas kernels  74.5 us (98%)
  local copies, waits for them, and re-layouts  1.67 us (2%)
    pallas_call x1, Pallas kernels, layer(): pl.pallas_call(functools.partial(layer_kernel, sizes), out_shape=jax.Shap...  74.5 us
    unnamed x1, local copies, waits for them, and re-layouts  1.67 us

profile of v3, /device:TPU:0, one launch (start us, length us, event | category | flops | bytes accessed | tf_op | source)
XLA Modules:
  0.0 76.2 jit_solution(14824642088815805353)
XLA Ops:
  0.0 74.5 %layer.1 = bf16[128,1024]{1,0:T(8,128)(2,1)} custom-call(bf16[128,1024]{1,0:T(8,128)(2,1)} %x_hbm.1, s32[8,128]{1,0:T(8,128)} %bitcast.2, f32[8,128]{1,0:T(8,128)} %bitcast.3, bf16[2,4096,384]{2,1,0:T(8,128)(2,1)} %gate_hbm.1, bf16[2,4096,384]{2,1,0:T(8,128)(2,1)} %up_hbm.1, bf16[2,384,4096]{2,1,0:T(8,128)(2,1)} %down_hbm.1), custom_call_target="tpu_custom_call" | custom-call | tf_op jit(solution)/shard_map/layer/pallas_call | solution.py:545
  74.5 1.7 %copy.8 = bf16[128,1024]{1,0:T(8,128)(2,1)} copy(bf16[128,1024]{1,0:T(8,128)(2,1)} %layer.1) | data formatting | bytes 524288

commit v4 on v3

--- a/solution.py
+++ b/solution.py
@@ -298,7 +298,7 @@
                     push(local(h, a, b, s, 1), piece_c(h, a, b, s), recv_c.at[a, b, s], there)
         for e in es:
             for f in range(2):
-                push(local_late(e, f, s, 1), late_c.at[s, e, f], recv_lc.at[s], there)
+                push(local_late(e, f, s, 1), late_c.at[s, e, f], recv_lc.at[s, es[0]], there)
 
     def add(dst, *srcs):
         chunk = 16
@@ -342,12 +342,13 @@
             else:
                 add(out_ref.at[pl.ds(*spans[h]), :], *srcs)
 
-    def late_out(s):
+    def late_out(s, es=(0, 1)):
         more = {0: (0, 2), 3: (1,)}.get(s, ())
-        arrive_rows(4 * tail, recv_lc.at[s])
+        arrive_rows(2 * len(es) * tail, recv_lc.at[s, es[0]])
         for k in more:
-            arrive_rows(4 * tail, recv_lz.at[k])
-        for e in range(2):
+            if es[-1]:
+                arrive_rows(4 * tail, recv_lz.at[k])
+        for e in es:
             for f in range(2):
                 piece = late_c.at[s, e, f]
                 add(piece, piece, local_late(e, f, s, 0), *[late_zs.at[k, e, f] for k in more])
@@ -427,21 +428,22 @@
     down(0, 1)
     swap(0)
     down(0, 0)
+    pass_last(1)
     late_meet(1)
-    pass_last(1)
     whole(1)
     hidden(1, 0)
     late_relay(2)
-    late_meet(2)
     pass_last(2)
     hidden(1, 1)
     pass_second(3)
+    step_first(0, 1)
+    late_meet(2)
     down(1, 1)
     swap(1)
     down(1, 0)
-    step_first(1, 1)
     whole(2)
     hidden(2, 1)
+    step_first(1, 1)
     step_first(1, 0)
     hidden(2, 0)
     late_meet(3)
@@ -452,30 +454,30 @@
     down(2, 0)
     step_first(2, 1)
     step_first(2, 0)
+    late_out(2)
     whole(3)
     hidden(3, 1)
-    late_out(2)
     down(3, 1, (1,))
     swap(3, (1,))
     down(3, 0, (1,))
     hidden(3, 0)
     step_second(2)
     step_first(3, 1)
+    late_out(3, (1,))
     down(3, 1, (0,))
     swap(3, (0,))
     down(3, 0, (0,))
     step_first(3, 0)
-    late_out(3)
+    late_out(3, (0,))
     step_last(2)
     step_second(3)
     step_second(1)
-    step_first(0, 1)
     step_first(0, 0)
+    step_second(0)
     step_last(3)
     late_out(0)
     late_first()
     step_last(1)
-    step_second(0)
     late_next()
     step_last(0)
     late_last()
@@ -490,8 +492,8 @@
 
 
 def cuts_of(rows):
-    late = 16
-    most = 64
+    late = 32
+    most = 48
     return [(0, most), (most, rows - late - most)] + ([(rows - late, late)] if late else [])
 
 
@@ -536,7 +538,7 @@
     ]
     semaphores = [pltpu.SemaphoreType.DMA(shape) for shape in (
         (4 + 3 * members,), (12,), (3, 3 * nz), (3, nz), (nz,), (nz,), (), (2, 2, nz), (2, 2, nz), (2, nz), (2, nz - 1),
-        (nz,), (nz - 1,), (tail // 16, 2), (tail // 16,))]
+        (nz, 2), (nz - 1,), (tail // 16, 2), (tail // 16,))]
     return buffers, semaphores
 
 

time: 76.3 us -> 74.3 us (0.974)
  Pallas kernels: 74.5 us -> 72.4 us
    pallas_call x1, Pallas kernels: 74.5 us -> 72.4 us  [layer(): pl.pallas_call(functools.partial(layer_kernel, sizes), out_shape=jax.Shap...]
where the time goes in v4:
time: 74.3 us; the launch traced here: 74.1 us
  Pallas kernels  72.4 us (97%)
  local copies, waits for them, and re-layouts  1.67 us (2%)
    pallas_call x1, Pallas kernels, layer(): pl.pallas_call(functools.partial(layer_kernel, sizes), out_shape=jax.Shap...  72.4 us
    unnamed x1, local copies, waits for them, and re-layouts  1.67 us

profile of v4, /device:TPU:0, one launch (start us, length us, event | category | flops | bytes accessed | tf_op | source)
XLA Modules:
  0.0 74.1 jit_solution(18365945864025558502)
XLA Ops:
  0.0 72.4 %layer.1 = bf16[128,1024]{1,0:T(8,128)(2,1)} custom-call(bf16[128,1024]{1,0:T(8,128)(2,1)} %x_hbm.1, s32[8,128]{1,0:T(8,128)} %bitcast.2, f32[8,128]{1,0:T(8,128)} %bitcast.3, bf16[2,4096,384]{2,1,0:T(8,128)(2,1)} %gate_hbm.1, bf16[2,4096,384]{2,1,0:T(8,128)(2,1)} %up_hbm.1, bf16[2,384,4096]{2,1,0:T(8,128)(2,1)} %down_hbm.1), custom_call_target="tpu_custom_call" | custom-call | tf_op jit(solution)/shard_map/layer/pallas_call | solution.py:547
  72.5 1.7 %copy.8 = bf16[128,1024]{1,0:T(8,128)(2,1)} copy(bf16[128,1024]{1,0:T(8,128)(2,1)} %layer.1) | data formatting | bytes 524288
